TPU v7x, 16 devices: a whole 2x2x2 slice. The times are simulated.
16 devices in a mesh: rep: 1, dp: 16 (over x, y, z, core).
Axes of the slice: x: 2, y: 2, z: 2, core: 2. Of those that a mesh axis runs over, the one named last changes fastest.
Arguments:
- a: bfloat16 [16, 4, 4096, 1024], P(('rep', 'dp'))
- g: bfloat16 [16, 4, 4096, 4096], P(('rep', 'dp'))
Outputs:
- output: bfloat16 [4, 1024, 4096], P('rep')
All inputs are finite; a program needn't handle non-finite values.
Results may differ from a plain program's by a relative error of at most 0.012.
Values are sent between devices in bfloat16 or wider.
A program may use at most 2 GiB of HBM per device.

v0:
```python
import jax
import jax.numpy as jnp


def solution(mesh):
    groups = mesh.shape["rep"]

    def step(a, g):
        a, g = (t.reshape(groups, -1, *t.shape[1:]) for t in (a, g))
        sums = jnp.einsum("rsntd,rsntf->rndf", a, g, preferred_element_type=jnp.float32)
        return sums.astype(jnp.bfloat16).reshape(-1, *sums.shape[2:])

    return step
```

profile of v0, /device:TPU:0, one launch (start us, length us, event | category | flops | bytes accessed | tf_op | source)
XLA Modules:
  0.0 764.3 jit_solution(10763280599418860599)
XLA Ops:
  0.0 150.8 %fusion = f32[4,1024,4096]{2,1,0:T(8,128)} fusion(bf16[1,4,4096,4096]{3,2,1,0:T(8,128)(2,1)} %param.1, bf16[1,4,4096,1024]{3,2,1,0:T(8,128)(2,1)} %param), kind=kOutput, calls=%fused_computation | convolution fusion | flops 137438953472 | bytes 234881024 | tf_op jit(solution)/rsntd,rsntf->rndf/dot_general | solution.py:10
  150.8 613.5 %all-reduce.2 = bf16[4,1024,4096]{2,1,0:T(8,128)(2,1)} all-reduce(f32[4,1024,4096]{2,1,0:T(8,128)} %fusion), channel_id=1, replica_groups=mesh['axis_0'=16] {'axis_0'}, use_global_device_ids=true, to_apply=%add.clone | all-reduce | flops 16777216 | bytes 100663296 | tf_op jit(solution)/rsntd,rsntf->rndf/dot_general | solution.py:10
where the time goes:
time: 764 us
  blocking collectives  613 us (80%)
  matrix products  151 us (20%)
    dot_general x1, blocking collectives, step(): jnp.einsum('rsntd,rsntf->rndf', a, g, preferred_element_type=jnp.float32)  613 us
    dot_general x1, matrix products, step(): jnp.einsum('rsntd,rsntf->rndf', a, g, preferred_element_type=jnp.float32)  151 us

commit v1 on v0

v1 whole, which is shorter than its diff:
```python
import functools

import jax
import jax.numpy as jnp
from jax import lax
from jax.experimental import pallas as pl
from jax.experimental.pallas import tpu as pltpu
from jax.sharding import PartitionSpec as P

MESH = pl.DeviceIdType.MESH
BF16, F32 = jnp.bfloat16, jnp.float32

MATS, TOKENS, D, F = 4, 4096, 1024, 4096
FB = 512
NJ = F // FB
NCH = MATS * NJ
VLIM = 26 * 2**20
NB = 256
HALF = D // 2
SR = 6
SS = 3
R, ROT = 2, 1
LAG = 3
NUM, DEN, T0 = 3, 3, 3 * R + 1


def kernel(a_hbm, g_hbm, out0, out1, abuf, gbuf, acc, sbuf, rbuf, k1, k2, k3, s1, s2, s3, r1, r2, r3,
           asem, gsem, dsend, drecv, rsend, rrecv, gsend, grecv):
    me = lax.axis_index("dp")
    core = me % 2
    bits = [(me // 8) % 2, (me // 4) % 2, (me // 2) % 2]
    mates = [me + (1 - 2 * b) * w for b, w in zip(bits, (8, 4, 2))]
    twin = me + 1 - 2 * core
    own = core * HALF

    def pick(which, values):
        return jnp.where(which == 0, values[0], jnp.where(which == 1, values[1], values[2]))

    def order(c, step):
        axis = (ROT * c + core + step) % 3
        return pick(axis, bits), pick(axis, mates)

    def remote(src, dst, send, recv, to):
        return pltpu.make_async_remote_copy(
            src_ref=src, dst_ref=dst, send_sem=send, recv_sem=recv, device_id={"dp": to}, device_id_type=MESH
        )

    def place(c):
        return c // NJ, pl.multiple_of((c % NJ) * FB, FB)

    def load_a(n, half):
        col = pl.multiple_of(jnp.where(half == 0, HALF - own, own), HALF)
        return pltpu.make_async_copy(a_hbm.at[n, :, pl.ds(col, HALF)], abuf.at[half], asem.at[half])

    def load_g(c):
        n, col = place(c)
        return pltpu.make_async_copy(g_hbm.at[n, :, pl.ds(col, FB)], gbuf.at[c % 2], gsem.at[c % 2])

    def twin_copy(c):
        return remote(sbuf.at[c % 2], rbuf.at[c % 2], dsend.at[c % 2], drecv.at[c % 2], twin)

    def scatter_copy(c, step):
        _, to = order(c, step)
        src, dst = ((s1, r1), (s2, r2), (s3, r3))[step]
        return remote(src.at[c % SS], dst.at[c % SR], rsend.at[step, c % SS], rrecv.at[step, c % SR], to)

    def piece(c):
        b1, b2, b3 = (order(c, s)[0] for s in range(3))
        return b1, b2, b3

    def rows_of(c, step):
        b1, b2, b3 = piece(c)
        if step == 0:
            return pl.ds(pl.multiple_of(own + b1 * 256 + b2 * 128 + b3 * 64, 64), 64)
        if step == 1:
            return pl.ds(pl.multiple_of(own + b1 * 256 + b2 * 128, 128), 128)
        if step == 2:
            return pl.ds(pl.multiple_of(own + b1 * 256, 256), 256)
        return pl.ds(pl.multiple_of(own, HALF), HALF)

    def gather_copy(c, step, out=out0, m=0):
        _, col = place(c)
        to = twin if step == 3 else order(c, 2 - step)[1]
        where = out.at[m, rows_of(c, step), pl.ds(col, FB)]
        return remote(where, where, gsend.at[step, c], grecv.at[step, c], to)

    def on_out(c, do):
        @pl.when(c < NJ)
        def _():
            do(out0, 0)

        @pl.when(c >= NJ)
        def _():
            do(out1, c // NJ - 1)

    def dots(c, half, store):
        for j in range(FB // NB):
            cols = slice(j * NB, (j + 1) * NB)
            store(cols, lax.dot_general(
                abuf[half], gbuf[c % 2, :, cols], (((0,), (0,)), ((), ())), preferred_element_type=F32))

    def store_send(c):
        def store(cols, x):
            sbuf[c % 2, :, cols] = x.astype(BF16)
        return store

    def store_own(cols, x):
        acc[:, cols] = x

    def halves(c, step, size):
        b, _ = order(c, step)
        return (pl.ds(pl.multiple_of((1 - b) * size, size), size), pl.ds(pl.multiple_of(b * size, size), size))

    def split(c, step, mine, theirs, send, keep, size):
        away, stay = halves(c, step, size)
        @pl.when(c >= SS)
        def _():
            scatter_copy(c - SS, step).wait_send()
        send[c % SS] = (mine[away] + theirs[away].astype(F32)).astype(BF16)
        scatter_copy(c, step).start()
        keep[c % R] = mine[stay] + theirs[stay].astype(F32)

    def reduce_round(t):
        c = t - 3 * R
        @pl.when((c >= 0) & (c < NCH))
        def _():
            scatter_copy(c, 2).wait_recv()
            _, col = place(c)
            total = (k3[c % R] + r3[c % SR].astype(F32)).astype(BF16)
            def put(out, m):
                out[m, rows_of(c, 0), pl.ds(col, FB)] = total
            on_out(c, put)
        for step, c, mine, recv, send, keep, size in (
            (2, t - 2 * R, k2, r2, s3, k3, 64),
            (1, t - R, k1, r1, s2, k2, 128),
        ):
            @pl.when((c >= 0) & (c < NCH))
            def _():
                scatter_copy(c, step - 1).wait_recv()
                split(c, step, mine.at[c % R], recv.at[c % SR], send, keep, size)
        @pl.when(t < NCH)
        def _():
            twin_copy(t).wait_recv()
            split(t, 0, acc, rbuf.at[t % 2], s1, k1, 256)

    def gather_round(u):
        for step in (3, 2, 1, 0):
            c = u - LAG * step
            @pl.when((c >= 0) & (c < NCH))
            def _():
                if step:
                    gather_copy(c, step - 1).wait_recv()
                on_out(c, lambda out, m: gather_copy(c, step, out, m).start())

    def rounds_before(t):
        return jnp.maximum(t - T0, 0) * NUM // DEN

    for half in range(2):
        load_a(0, half).start()
    load_g(0).start()

    barrier = pltpu.get_barrier_semaphore()
    for to in (*mates, twin):
        pl.semaphore_signal(barrier, inc=1, device_id={"dp": to}, device_id_type=MESH)
    pl.semaphore_wait(barrier, 4)

    @pl.loop(0, NCH)
    def _(t):
        n, j = t // NJ, t % NJ
        load_g(t).wait()
        @pl.when(t + 1 < NCH)
        def _():
            load_g(t + 1).start()
        for half in range(2):
            @pl.when(j == 0)
            def _():
                load_a(n, half).wait()
            if half == 0:
                @pl.when(t >= 2)
                def _():
                    twin_copy(t - 2).wait_send()
                dots(t, 0, store_send(t))
                twin_copy(t).start()
            else:
                dots(t, 1, store_own)
            @pl.when((j == NJ - 1) & (n < MATS - 1))
            def _():
                load_a(n + 1, half).start()
        reduce_round(t)
        u = rounds_before(t)
        @pl.when(rounds_before(t + 1) > u)
        def _():
            gather_round(u)

    first = max(NCH - T0, 0) * NUM // DEN

    @pl.loop(first, NCH + 3 * LAG)
    def _(u):
        t = u - first + NCH
        @pl.when(t < NCH + 3 * R)
        def _():
            reduce_round(t)
        gather_round(u)

    for c in range(NCH - 2, NCH):
        twin_copy(c).wait_send()
    for step in range(3):
        for c in range(NCH - SS, NCH):
            scatter_copy(c, step).wait_send()

    @pl.loop(0, NCH)
    def _(c):
        for step in range(4):
            gather_copy(c, step).wait_send()
        gather_copy(c, 3).wait_recv()


def gather_up(out0, out1, out, sem):
    copies = [
        pltpu.make_async_copy(src, out.at[n], sem.at[n])
        for n, src in enumerate((out0.at[0], out1.at[0], out1.at[1], out1.at[2]))
    ]
    for copy in copies:
        copy.start()
    for copy in copies:
        copy.wait()


def solution(mesh):
    def body(a, g):
        vmem = pltpu.VMEM
        dma = pltpu.SemaphoreType.DMA
        hbm, near = pl.BlockSpec(memory_space=pl.ANY), pl.BlockSpec(memory_space=vmem)
        parts = pl.pallas_call(
            kernel,
            name="sums",
            out_shape=[vmem((1, D, F), BF16), vmem((MATS - 1, D, F), BF16)],
            in_specs=[hbm] * 2,
            out_specs=[near] * 2,
            scratch_shapes=[
                vmem((2, TOKENS, HALF), BF16),
                vmem((2, TOKENS, FB), BF16),
                vmem((HALF, FB), F32),
                vmem((2, HALF, FB), BF16),
                vmem((2, HALF, FB), BF16),
                vmem((R, 256, FB), F32),
                vmem((R, 128, FB), F32),
                vmem((R, 64, FB), F32),
                vmem((SS, 256, FB), BF16),
                vmem((SS, 128, FB), BF16),
                vmem((SS, 64, FB), BF16),
                vmem((SR, 256, FB), BF16),
                vmem((SR, 128, FB), BF16),
                vmem((SR, 64, FB), BF16),
                dma((2,)), dma((2,)), dma((2,)), dma((2,)),
                dma((3, SS)), dma((3, SR)),
                dma((4, NCH)), dma((4, NCH)),
            ],
            compiler_params=pltpu.CompilerParams(
                collective_id=0, has_side_effects=True, vmem_limit_bytes=VLIM
            ),
        )(a[0], g[0])
        return pl.pallas_call(
            gather_up,
            name="gather_up",
            out_shape=jax.ShapeDtypeStruct((MATS, D, F), BF16),
            in_specs=[near] * 2,
            out_specs=hbm,
            scratch_shapes=[dma((4,))],
            compiler_params=pltpu.CompilerParams(vmem_limit_bytes=2**20),
        )(*parts)

    return jax.shard_map(
        body, mesh=mesh, in_specs=P(("rep", "dp")), out_specs=P("rep"), check_vma=False
    )
```

time: 764 us -> 263 us (0.34)
  blocking collectives: 613 us -> 0 us
  Pallas kernels: 0 us -> 263 us
  matrix products: 151 us -> 0 us
    dot_general x1 -> x0, blocking collectives: 613 us -> none  [step(): jnp.einsum('rsntd,rsntf->rndf', a, g, preferred_element_type=jnp.float32)]
    pallas_call x0 -> x2, Pallas kernels: none -> 263 us  [the longest x1 252 us: body(): pl.pallas_call(kernel, name='sums', out_shape=[vmem((1, D, F), BF16), vme...]
    dot_general x1 -> x0, matrix products: 151 us -> none  [step(): jnp.einsum('rsntd,rsntf->rndf', a, g, preferred_element_type=jnp.float32)]
where the time goes in v1:
time: 263 us
  Pallas kernels  263 us (100%)
    pallas_call x1, Pallas kernels, body(): pl.pallas_call(kernel, name='sums', out_shape=[vmem((1, D, F), BF16), vme...  252 us
    pallas_call x1, Pallas kernels, body(): pl.pallas_call(gather_up, name='gather_up', out_shape=jax.ShapeDtypeStruc...  11.2 us

profile of v1, /device:TPU:0, one launch (start us, length us, event | category | flops | bytes accessed | tf_op | source)
XLA Modules:
  0.0 262.9 jit_solution(17162002898416176036)
XLA Ops:
  0.0 251.6 %sums.1 = (bf16[1,1024,4096]{2,1,0:T(8,128)(2,1)S(1)}, bf16[3,1024,4096]{2,1,0:T(8,128)(2,1)S(1)}) custom-call(bf16[4,4096,1024]{2,1,0:T(8,128)(2,1)} %bitcast.2, bf16[4,4096,4096]{2,1,0:T(8,128)(2,1)} %bitcast.1.g_hbm), custom_call_target="tpu_custom_call" | custom-call | tf_op jit(solution)/shard_map/sums/pallas_call | solution.py:234
  251.7 11.2 %gather_up.1 = bf16[4,1024,4096]{2,1,0:T(8,128)(2,1)} custom-call(bf16[1,1024,4096]{2,1,0:T(8,128)(2,1)S(1)} %get-tuple-element.7.out0, bf16[3,1024,4096]{2,1,0:T(8,128)(2,1)S(1)} %get-tuple-element.8.out1), custom_call_target="tpu_custom_call" | custom-call | tf_op jit(solution)/shard_map/gather_up/pallas_call | solution.py:263

commit v2 on v1

v2 whole, which is shorter than its diff:
```python
import functools

import jax
import jax.numpy as jnp
from jax import lax
from jax.experimental import pallas as pl
from jax.experimental.pallas import tpu as pltpu
from jax.sharding import PartitionSpec as P

MESH = pl.DeviceIdType.MESH
BF16, F32 = jnp.bfloat16, jnp.float32

MATS, TOKENS, D, F = 4, 4096, 1024, 4096
FB = 512
RB = 256
NJ, NH = F // FB, D // 2 // RB
NM = NJ * NH
NCH = MATS * NM
VLIM = 26 * 2**20
NB = 512
HALF = D // 2
SR = 6
SS = 3
R, ROT = 2, 1
LAG = 3
T0 = 3 * R


class At:
    def __init__(self, value, rest):
        self.value, self.rest = value, rest % 6

    def __sub__(self, k):
        return At(self.value - k, self.rest - k)

    def __mod__(self, k):
        assert 6 % k == 0
        return self.rest % k


def kernel(a_hbm, g_hbm, out0, out1, abuf, gbuf, acc, sbuf, rbuf, k1, k2, k3, s1, s2, s3, r1, r2, r3,
           asem, gsem, dsend, drecv, rsend, rrecv, gsend, grecv):
    me = lax.axis_index("dp")
    core = me % 2
    bits = [(me // 8) % 2, (me // 4) % 2, (me // 2) % 2]
    mates = [me + (1 - 2 * b) * w for b, w in zip(bits, (8, 4, 2))]
    twin = me + 1 - 2 * core
    own = core * HALF

    def pick(which, values):
        return jnp.where(which == 0, values[0], jnp.where(which == 1, values[1], values[2]))

    ways = [(pick((k + core) % 3, bits), pick((k + core) % 3, mates)) for k in range(3)]

    def order(c, step):
        return ways[(ROT * c.rest + step) % 3]

    def remote(src, dst, send, recv, to):
        return pltpu.make_async_remote_copy(
            src_ref=src, dst_ref=dst, send_sem=send, recv_sem=recv, device_id={"dp": to}, device_id_type=MESH
        )

    def place(c):
        c = c.value
        return c // NM, pl.multiple_of((c % NM) // NH * FB, FB), pl.multiple_of(own + c % NH * RB, RB)

    def load_a(n, half):
        col = pl.multiple_of(jnp.where(half == 0, HALF - own, own), HALF)
        return pltpu.make_async_copy(a_hbm.at[n, :, pl.ds(col, HALF)], abuf.at[half], asem.at[half])

    def load_g(c):
        n, col, _ = place(c)
        slot = c.value // NH % 2
        return pltpu.make_async_copy(g_hbm.at[n, :, pl.ds(col, FB)], gbuf.at[slot], gsem.at[slot])

    def twin_copy(c):
        return remote(sbuf.at[c % 2], rbuf.at[c % 2], dsend.at[c % 2], drecv.at[c % 2], twin)

    def scatter_copy(c, step):
        _, to = order(c, step)
        src, dst = ((s1, r1), (s2, r2), (s3, r3))[step]
        return remote(src.at[c % SS], dst.at[c % SR], rsend.at[step, c % SS], rrecv.at[step, c % SR], to)

    def piece(c):
        b1, b2, b3 = (order(c, s)[0] for s in range(3))
        return b1, b2, b3

    def rows_of(c, step):
        b1, b2, b3 = piece(c)
        base = place(c)[2]
        if step == 0:
            return pl.ds(pl.multiple_of(base + b1 * (RB // 2) + b2 * (RB // 4) + b3 * (RB // 8), RB // 8), RB // 8)
        if step == 1:
            return pl.ds(pl.multiple_of(base + b1 * (RB // 2) + b2 * (RB // 4), RB // 4), RB // 4)
        if step == 2:
            return pl.ds(pl.multiple_of(base + b1 * (RB // 2), RB // 2), RB // 2)
        return pl.ds(base, RB)

    def gather_copy(c, step, out=out0, m=0):
        _, col, _ = place(c)
        to = twin if step == 3 else order(c, 2 - step)[1]
        where = out.at[m, rows_of(c, step), pl.ds(col, FB)]
        return remote(where, where, gsend.at[step, c.value], grecv.at[step, c.value], to)

    def on_out(c, do):
        @pl.when(c.value < NM)
        def _():
            do(out0, 0)

        @pl.when(c.value >= NM)
        def _():
            do(out1, c.value // NM - 1)

    def dots(c, half, store):
        for j in range(FB // NB):
            cols = slice(j * NB, (j + 1) * NB)
            store(cols, lax.dot_general(
                abuf[half, :, pl.ds(c % NH * RB, RB)], gbuf[c.value // NH % 2, :, cols], (((0,), (0,)), ((), ())), preferred_element_type=F32))

    def store_send(c):
        def store(cols, x):
            sbuf[c % 2, :, cols] = x.astype(BF16)
        return store

    def store_own(cols, x):
        acc[:, cols] = x

    def halves(c, step, size):
        b, _ = order(c, step)
        return (pl.ds(pl.multiple_of((1 - b) * size, size), size), pl.ds(pl.multiple_of(b * size, size), size))

    def split(c, step, mine, theirs, send, keep, size):
        away, stay = halves(c, step, size)
        @pl.when(c.value >= SS)
        def _():
            scatter_copy(c - SS, step).wait_send()
        send[c % SS] = (mine[away] + theirs[away].astype(F32)).astype(BF16)
        scatter_copy(c, step).start()
        keep[c % R] = mine[stay] + theirs[stay].astype(F32)

    def reduce_round(t):
        c = t - 3 * R
        @pl.when((c.value >= 0) & (c.value < NCH))
        def _():
            scatter_copy(c, 2).wait_recv()
            _, col, _ = place(c)
            total = (k3[c % R] + r3[c % SR].astype(F32)).astype(BF16)
            def put(out, m):
                out[m, rows_of(c, 0), pl.ds(col, FB)] = total
            on_out(c, put)
        for step, c, mine, recv, send, keep, size in (
            (2, t - 2 * R, k2, r2, s3, k3, RB // 8),
            (1, t - R, k1, r1, s2, k2, RB // 4),
        ):
            @pl.when((c.value >= 0) & (c.value < NCH))
            def _():
                scatter_copy(c, step - 1).wait_recv()
                split(c, step, mine.at[c % R], recv.at[c % SR], send, keep, size)
        @pl.when(t.value < NCH)
        def _():
            twin_copy(t).wait_recv()
            split(t, 0, acc, rbuf.at[t % 2], s1, k1, RB // 2)

    def gather_round(u):
        for step in (3, 2, 1, 0):
            c = u - LAG * step
            @pl.when((c.value >= 0) & (c.value < NCH))
            def _():
                if step:
                    gather_copy(c, step - 1).wait_recv()
                on_out(c, lambda out, m: gather_copy(c, step, out, m).start())

    for half in range(2):
        load_a(0, half).start()
    load_g(At(0, 0)).start()

    barrier = pltpu.get_barrier_semaphore()
    for to in (*mates, twin):
        pl.semaphore_signal(barrier, inc=1, device_id={"dp": to}, device_id_type=MESH)
    pl.semaphore_wait(barrier, 4)

    def multiply(t):
        n, j = t.value // NM, t.value % NM

        if t % NH == 0:
            load_g(t).wait()

            @pl.when(t.value + NH < NCH)
            def _():
                load_g(t - -NH).start()

        for half in range(2):
            @pl.when(j == 0)
            def _():
                load_a(n, half).wait()
            if half == 0:
                @pl.when(t.value >= 2)
                def _():
                    twin_copy(t - 2).wait_send()
                dots(t, 0, store_send(t))
                twin_copy(t).start()
            else:
                dots(t, 1, store_own)
            @pl.when((j == NM - 1) & (n < MATS - 1))
            def _():
                load_a(n + 1, half).start()

    @pl.loop(0, pl.cdiv(max(NCH + 3 * R, NCH + T0 + 3 * LAG), 6))
    def _(q):
        for r in range(6):
            t = At(6 * q + r, r)

            @pl.when(t.value < NCH)
            def _():
                multiply(t)
            reduce_round(t)
            gather_round(t - T0)

    for c in range(NCH - 2, NCH):
        twin_copy(At(c, c)).wait_send()
    for step in range(3):
        for c in range(NCH - SS, NCH):
            scatter_copy(At(c, c), step).wait_send()

    @pl.loop(0, NCH)
    def _(c):
        for step in range(4):
            gather_copy(At(c, 0), step).wait_send()
        gather_copy(At(c, 0), 3).wait_recv()


def gather_up(out0, out1, out, sem):
    copies = [
        pltpu.make_async_copy(src, out.at[n], sem.at[n])
        for n, src in enumerate((out0.at[0], out1.at[0], out1.at[1], out1.at[2]))
    ]
    for copy in copies:
        copy.start()
    for copy in copies:
        copy.wait()


def solution(mesh):
    def body(a, g):
        vmem = pltpu.VMEM
        dma = pltpu.SemaphoreType.DMA
        hbm, near = pl.BlockSpec(memory_space=pl.ANY), pl.BlockSpec(memory_space=vmem)
        parts = pl.pallas_call(
            kernel,
            name="sums",
            out_shape=[vmem((1, D, F), BF16), vmem((MATS - 1, D, F), BF16)],
            in_specs=[hbm] * 2,
            out_specs=[near] * 2,
            scratch_shapes=[
                vmem((2, TOKENS, HALF), BF16),
                vmem((2, TOKENS, FB), BF16),
                vmem((RB, FB), F32),
                vmem((2, RB, FB), BF16),
                vmem((2, RB, FB), BF16),
                vmem((R, RB // 2, FB), F32),
                vmem((R, RB // 4, FB), F32),
                vmem((R, RB // 8, FB), F32),
                vmem((SS, RB // 2, FB), BF16),
                vmem((SS, RB // 4, FB), BF16),
                vmem((SS, RB // 8, FB), BF16),
                vmem((SR, RB // 2, FB), BF16),
                vmem((SR, RB // 4, FB), BF16),
                vmem((SR, RB // 8, FB), BF16),
                dma((2,)), dma((2,)), dma((2,)), dma((2,)),
                dma((3, SS)), dma((3, SR)),
                dma((4, NCH)), dma((4, NCH)),
            ],
            compiler_params=pltpu.CompilerParams(
                collective_id=0, has_side_effects=True, vmem_limit_bytes=VLIM
            ),
        )(a[0], g[0])
        return pl.pallas_call(
            gather_up,
            name="gather_up",
            out_shape=jax.ShapeDtypeStruct((MATS, D, F), BF16),
            in_specs=[near] * 2,
            out_specs=hbm,
            scratch_shapes=[dma((4,))],
            compiler_params=pltpu.CompilerParams(vmem_limit_bytes=2**20),
        )(*parts)

    return jax.shard_map(
        body, mesh=mesh, in_specs=P(("rep", "dp")), out_specs=P("rep"), check_vma=False
    )
```

time: 263 us -> 254 us (0.966)
  Pallas kernels: 263 us -> 253 us
    pallas_call x1, Pallas kernels: 252 us -> 242 us  [body(): pl.pallas_call(kernel, name='sums', out_shape=[vmem((1, D, F), BF16), vme...]
where the time goes in v2:
time: 254 us; the launch traced here: 253 us
  Pallas kernels  253 us (100%)
    pallas_call x1, Pallas kernels, body(): pl.pallas_call(kernel, name='sums', out_shape=[vmem((1, D, F), BF16), vme...  242 us
    pallas_call x1, Pallas kernels, body(): pl.pallas_call(gather_up, name='gather_up', out_shape=jax.ShapeDtypeStruc...  11.2 us

profile of v2, /device:TPU:0, one launch (start us, length us, event | category | flops | bytes accessed | tf_op | source)
XLA Modules:
  0.0 253.5 jit_solution(15634234275712288438)
XLA Ops:
  0.0 242.2 %sums.1 = (bf16[1,1024,4096]{2,1,0:T(8,128)(2,1)S(1)}, bf16[3,1024,4096]{2,1,0:T(8,128)(2,1)S(1)}) custom-call(bf16[4,4096,1024]{2,1,0:T(8,128)(2,1)} %bitcast.2, bf16[4,4096,4096]{2,1,0:T(8,128)(2,1)} %bitcast.1.g_hbm), custom_call_target="tpu_custom_call" | custom-call | tf_op jit(solution)/shard_map/sums/pallas_call | solution.py:248
  242.2 11.2 %gather_up.1 = bf16[4,1024,4096]{2,1,0:T(8,128)(2,1)} custom-call(bf16[1,1024,4096]{2,1,0:T(8,128)(2,1)S(1)} %get-tuple-element.7.out0, bf16[3,1024,4096]{2,1,0:T(8,128)(2,1)S(1)} %get-tuple-element.8.out1), custom_call_target="tpu_custom_call" | custom-call | tf_op jit(solution)/shard_map/gather_up/pallas_call | solution.py:277
